TPU v7x, 32 devices: a whole 2x2x4 slice. The times are simulated.
32 devices in a mesh: tm: 8 (over z, y), obs: 4 (over x, core).
Axes of the slice: x: 2, y: 2, z: 4, core: 2. Of those that a mesh axis runs over, the one named last changes fastest.
Arguments:
- trajectory: bfloat16 [8, 64, 256, 128], P('tm', 'obs'), may hold values from -6 to 6
- weights: bfloat16 [1024, 128, 256], P(('tm', 'obs')), may hold values from -0.375 to 0.375
- observed: bfloat16 [1024, 128, 128], P(('tm', 'obs')), may hold values from -9 to 9
- window: int32 [1024, 1], P(('tm', 'obs')), may hold values from 0 to 7; in each aligned block of 32 rows (0 to 31, 32 to 63, ...) at most 4 rows name the same one
- block: int32 [1024], P(('tm', 'obs')), may hold values from 0 to 15
- counts: int32 [1024], P(('tm', 'obs')), may hold values from 32 to 128, as said below
- flags: int32 [1024, 128], P(('tm', 'obs')), may hold values 0 or 1
- inv_error: float32 [128], replicated, may hold values from 0.5 to 2
Outputs:
- departures: bfloat16 [1024, 128, 128], P(('tm', 'obs'))
- window_bias: float32 [8, 128], P('tm')
- window_chi: float32 [8, 128], P('tm')
Inputs may be any that keep to these rules, and one draw needn't show every extreme that they name: Among the 32 groups of one device, no sub-window is named by more than 4. `counts`: among the 32 groups of one device, one has all 128 slots live.
All inputs are finite; a program needn't handle non-finite values. No bound on the sum of `flags` on one device may be relied on, other than what follows from the above.
Results may differ from a plain program's by a relative error of at most 0.001.
Values may be sent and summed in bfloat16 or wider, within the bound.
A program may use at most 64 MiB of HBM per device.

v0:
```python
import functools

import jax
import jax.numpy as jnp
from jax import lax
from jax.experimental import pallas as pl
from jax.experimental.pallas import tpu as pltpu
from jax.sharding import PartitionSpec as P

GCAP = 4
MESH = pl.DeviceIdType.MESH


def flip(index, pattern):
    bit = 1
    moved = index
    while bit <= pattern:
        if pattern & bit:
            moved = moved + bit * (1 - 2 * ((index // bit) % 2))
        bit *= 2
    return moved


def phases(windows):
    half, quarter = windows // 2, max(1, windows // 4)
    far = list(range(half, windows))
    return far[:1] + list(range(quarter, half)) + far[1:] + list(range(1, quarter))


def last_hits(win_of, value_of, groups, wanted, start):
    def step(g, held):
        hit = win_of(g) == wanted
        shifted = (value_of(g),) + held[:-1]
        return tuple(jnp.where(hit, new, old) for new, old in zip(shifted, held))

    return lax.fori_loop(0, groups, step, (jnp.int32(start),) * GCAP, unroll=8)


def kernel(
    windows, regions, groups, slots, levels,
    traj, weights, observed, win_in, blk_in, counts_in, flags_in, inv_in,
    dep_out, total_out,
    slab, wts, obs, send, recv, mask, dep_slot, dep_v, stat_send, stat_recv,
    idx, own, table, slot_tab, counts, flags, inv,
    in_sems, out_sem, idx_send, idx_recv, dat_send, dat_recv, st_send, st_recv,
):
    me = lax.axis_index("tm")
    my_region = lax.axis_index("obs")
    everyone = windows * regions
    flat = me * regions + my_region
    order = phases(windows)

    small = [
        pltpu.make_async_copy(src, dst, in_sems.at[3 + n])
        for n, (src, dst) in enumerate(
            ((win_in, own.at[0]), (blk_in, own.at[1]), (counts_in, counts), (flags_in, flags), (inv_in, inv))
        )
    ]
    for copy in small:
        copy.start()
    slab_in = pltpu.make_async_copy(traj.at[0], slab, in_sems.at[0])
    slab_in.start()
    wts_in = pltpu.make_async_copy(weights, wts, in_sems.at[1])
    obs_in = pltpu.make_async_copy(observed, obs, in_sems.at[2])

    barrier = pltpu.get_barrier_semaphore()

    partners = [(flip(me, d), my_region) for d in order]
    partners += [(me, (my_region + r) % regions) for r in range(1, regions)]
    for partner in partners:
        pl.semaphore_signal(barrier, inc=1, device_id=partner, device_id_type=MESH)
    small[0].wait()
    small[1].wait()
    pl.semaphore_wait(barrier, len(partners))

    requests = []
    for j, d in enumerate(order):
        target = (flip(me, d), my_region)
        copy = pltpu.make_async_remote_copy(
            src_ref=own, dst_ref=idx.at[j],
            send_sem=idx_send.at[j], recv_sem=idx_recv.at[j],
            device_id=target, device_id_type=MESH,
        )
        copy.start()
        requests.append(copy)
    wts_in.start()
    obs_in.start()

    slab_in.wait()
    moves = []
    for j, d in enumerate(order):
        requests[j].wait_recv()
        named = last_hits(
            lambda g, j=j: idx[j, 0, g], lambda g, j=j: idx[j, 1, g], groups, me, 0
        )
        for k in range(GCAP):
            send[j * GCAP + k] = slab[named[k]]
        copy = pltpu.make_async_remote_copy(
            src_ref=send.at[pl.ds(j * GCAP, GCAP)],
            dst_ref=recv.at[pl.ds(j * GCAP, GCAP)],
            send_sem=dat_send.at[j], recv_sem=dat_recv.at[j],
            device_id=(flip(me, d), my_region), device_id_type=MESH,
        )
        copy.start()
        moves.append(copy)

    for copy in small[2:]:
        copy.wait()

    def fill(w, carry):
        named = last_hits(lambda g: own[0, g], lambda g: g, groups, w, -1)
        for k in range(GCAP):
            table[w * GCAP + k] = named[k]
        return carry

    lax.fori_loop(0, windows, fill, 0)

    def place(g, carry):
        base = own[0, g] * GCAP
        rank = jnp.int32(0)
        for k in range(1, GCAP):
            rank = rank + jnp.where(table[base + k] == g, k, 0)
        slot_tab[g] = base + rank
        return carry

    lax.fori_loop(0, groups, place, 0)

    down = lax.broadcasted_iota(jnp.int32, (slots, slots), 0)
    across = lax.broadcasted_iota(jnp.int32, (slots, slots), 1)
    lane = lax.broadcasted_iota(jnp.int32, (1, slots), 1)
    ones = jnp.ones((slots, levels), jnp.bfloat16)

    def spread(g, carry):
        row = jnp.where(lane < counts[g], flags[pl.ds(g, 1), :], 0)
        diagonal = jnp.where(down == across, jnp.broadcast_to(row, (slots, slots)), 0)
        mask[g] = jnp.dot(
            diagonal.astype(jnp.float32).astype(jnp.bfloat16), ones,
            preferred_element_type=jnp.float32,
        )
        return carry

    lax.fori_loop(0, groups, spread, 0)
    wts_in.wait()
    obs_in.wait()
    inverse = inv[...]
    padded = windows * GCAP > groups

    def check(w, blocks):
        one = jnp.zeros((1, levels), jnp.float32)
        two = jnp.zeros((1, levels), jnp.float32)
        kept = jnp.zeros((1, levels), jnp.float32)
        for k in range(GCAP):
            named = table[w * GCAP + k]
            g = jnp.maximum(named, 0)
            hx = jnp.dot(wts[g], blocks(k, g), preferred_element_type=jnp.float32)
            keep = mask[g]
            if padded:
                keep = keep * jnp.where(named >= 0, 1.0, 0.0)
            dep = keep * (obs[g].astype(jnp.float32) - hx) * inverse
            dep_slot[w * GCAP + k] = dep.astype(jnp.bfloat16)
            one = one + jnp.sum(dep, 0, keepdims=True)
            two = two + jnp.sum(dep * dep, 0, keepdims=True)
            kept = kept + jnp.sum(keep, 0, keepdims=True)
        stat_send[w] = jnp.concatenate(
            [one, two, kept, jnp.zeros((5, levels), jnp.float32)], 0
        )

    def share(w, first):
        for r in range(first, regions):
            copy = pltpu.make_async_remote_copy(
                src_ref=stat_send.at[w], dst_ref=stat_recv.at[flat],
                send_sem=st_send, recv_sem=st_recv,
                device_id=(w, (my_region + r) % regions), device_id_type=MESH,
            )
            copy.start()

    check(me, lambda k, g: slab[own[1, g]])
    share(me, 1)
    for j, d in sorted(enumerate(order), key=lambda item: item[1] >= windows // 2):
        w = flip(me, d)
        moves[j].wait_recv()
        check(w, lambda k, g, j=j: recv[j * GCAP + k])
        share(w, 0)

    def permute(g, carry):
        dep_v[g] = dep_slot[slot_tab[g]]
        return carry

    lax.fori_loop(0, groups, permute, 0, unroll=4)
    out = pltpu.make_async_copy(dep_v, dep_out, out_sem)
    out.start()

    for j in range(len(order)):
        requests[j].wait_send()
        moves[j].wait_send()

    rest = pl.ds(0, everyone - 1)
    arrived = pltpu.make_async_remote_copy(
        src_ref=stat_recv.at[rest], dst_ref=stat_recv.at[rest],
        send_sem=st_send, recv_sem=st_recv,
        device_id=(flip(me, 1), my_region), device_id_type=MESH,
    )
    arrived.wait_recv()
    stat_recv[flat] = stat_send[me]
    total_out[...] = jnp.sum(stat_recv[...], 0)
    arrived.wait_send()
    out.wait()


def per_device(trajectory, weights, observed, window, block, counts, flags, inv_error):
    windows = lax.axis_size("tm")
    regions = lax.axis_size("obs")
    groups, slots, columns = weights.shape
    levels = observed.shape[2]
    blocks = trajectory.shape[1]
    peers = windows - 1
    dma = pltpu.SemaphoreType.DMA
    hbm = pl.BlockSpec(memory_space=pl.ANY)
    vmem = pl.BlockSpec(memory_space=pltpu.VMEM)
    b16, f32, i32 = jnp.bfloat16, jnp.float32, jnp.int32
    departures, total = pl.pallas_call(
        functools.partial(kernel, windows, regions, groups, slots, levels),
        out_shape=(
            jax.ShapeDtypeStruct((groups, slots, levels), b16),
            jax.ShapeDtypeStruct((8, levels), f32),
        ),
        in_specs=[hbm] * 8,
        out_specs=(hbm, vmem),
        scratch_shapes=[
            pltpu.VMEM((blocks, columns, levels), b16),
            pltpu.VMEM((groups, slots, columns), b16),
            pltpu.VMEM((groups, slots, levels), b16),
            pltpu.VMEM((peers * GCAP, columns, levels), b16),
            pltpu.VMEM((peers * GCAP, columns, levels), b16),
            pltpu.VMEM((groups, slots, levels), f32),
            pltpu.VMEM((windows * GCAP, slots, levels), b16),
            pltpu.VMEM((groups, slots, levels), b16),
            pltpu.VMEM((windows, 8, levels), f32),
            pltpu.VMEM((windows * regions, 8, levels), f32),
            pltpu.SMEM((peers, 2, groups), i32),
            pltpu.SMEM((2, groups), i32),
            pltpu.SMEM((windows * GCAP,), i32),
            pltpu.SMEM((groups,), i32),
            pltpu.SMEM((groups,), i32),
            pltpu.VMEM((groups, slots), i32),
            pltpu.VMEM((1, levels), f32),
            dma((8,)),
            dma,
            dma((peers,)),
            dma((peers,)),
            dma((peers,)),
            dma((peers,)),
            dma,
            dma,
        ],
        compiler_params=pltpu.CompilerParams(
            collective_id=0, has_side_effects=True, vmem_limit_bytes=60 * 1024 * 1024
        ),
    )(
        trajectory, weights, observed, window[:, 0], block, counts, flags,
        inv_error.reshape(1, levels),
    )
    weight = total[2:3] + 1.0
    return (departures, total[0:1] / jnp.sqrt(weight), total[1:2] / weight)


def solution(mesh):
    return jax.shard_map(
        per_device,
        mesh=mesh,
        in_specs=(
            P("tm", "obs", None, None),
            P(("tm", "obs"), None, None),
            P(("tm", "obs"), None, None),
            P(("tm", "obs"), None),
            P(("tm", "obs")),
            P(("tm", "obs")),
            P(("tm", "obs"), None),
            P(),
        ),
        out_specs=(P(("tm", "obs"), None, None), P("tm", None), P("tm", None)),
        check_vma=False,
    )
```

profile of v0, /device:TPU:8, one launch (start us, length us, event | category | flops | bytes accessed | tf_op | source)
XLA Modules:
  0.0 63.0 jit_solution(1097231903453205090)
XLA Ops:
  0.6 58.8 %shard_map.103 = (bf16[32,128,128]{2,1,0:T(8,128)(2,1)}, f32[8,128]{1,0:T(8,128)}) custom-call(bf16[1,16,256,128]{3,2,1,0:T(8,128)(2,1)} %traj.1, bf16[32,128,256]{2,1,0:T(8,128)(2,1)} %weights.1, bf16[32,128,128]{2,1,0:T(8,128)(2,1)} %observed.1, s32[32]{0:T(128)} %bitcast.2, s32[32]{0:T(128)} %blk_in.1, s32[32]{0:T(128)} %counts_in.1, s32[32,128]{1,0:T(8,128)} %flags_in.1, ...), custom_call_target="tpu_custom_call" | custom-call | tf_op jit(solution)/shard_map/pallas_call | solution.py:221
  59.4 1.3 %slice_divide_fusion = (f32[1,128]{1,0:T(1,128)}, f32[1,128]{1,0:T(1,128)}) fusion(f32[8,128]{1,0:T(8,128)} %get-tuple-element.6), kind=kLoop, calls=%fused_computation | loop fusion | flops 384 | bytes 2560 | tf_op jit(solution)/shard_map/div | solution.py:264
  60.7 2.3 %copy.12 = bf16[32,128,128]{2,1,0:T(8,128)(2,1)} copy(bf16[32,128,128]{2,1,0:T(8,128)(2,1)} %get-tuple-element.12) | data formatting | bytes 2097152
where the time goes:
time: 64 us; the launch traced here: 63 us
  Pallas kernels  58.8 us (92%)
  local copies, waits for them, and re-layouts  2.31 us (4%)
  other arithmetic  1.31 us (2%)
  between operations  0.64 us (1%)
    pallas_call x1, Pallas kernels, per_device(): pl.pallas_call(functools.partial(kernel, windows, regions, groups, slots,...  58.8 us
    unnamed x1, local copies, waits for them, and re-layouts  2.31 us
    div x1, other arithmetic, per_device(): return (departures, total[0:1] / jnp.sqrt(weight), total[1:2] / weight)  1.31 us

commit v1 on v0

--- a/solution.py
+++ b/solution.py
@@ -187,8 +187,8 @@
         return carry
 
     lax.fori_loop(0, groups, permute, 0, unroll=4)
-    out = pltpu.make_async_copy(dep_v, dep_out, out_sem)
-    out.start()
+    dep_out[...] = dep_v[...]
+
 
     for j in range(len(order)):
         requests[j].wait_send()
@@ -204,7 +204,6 @@
     stat_recv[flat] = stat_send[me]
     total_out[...] = jnp.sum(stat_recv[...], 0)
     arrived.wait_send()
-    out.wait()
 
 
 def per_device(trajectory, weights, observed, window, block, counts, flags, inv_error):
@@ -221,11 +220,11 @@
     departures, total = pl.pallas_call(
         functools.partial(kernel, windows, regions, groups, slots, levels),
         out_shape=(
-            jax.ShapeDtypeStruct((groups, slots, levels), b16),
-            jax.ShapeDtypeStruct((8, levels), f32),
+            pltpu.VMEM((groups, slots, levels), b16),
+            pltpu.VMEM((8, levels), f32),
         ),
         in_specs=[hbm] * 8,
-        out_specs=(hbm, vmem),
+        out_specs=(vmem, vmem),
         scratch_shapes=[
             pltpu.VMEM((blocks, columns, levels), b16),
             pltpu.VMEM((groups, slots, columns), b16),

time: 64 us -> 61.3 us (0.958)
  local copies, waits for them, and re-layouts: 2.31 us -> 0.97 us
  other arithmetic: 1.31 us -> 0.53 us
    unnamed x1, local copies, waits for them, and re-layouts: 2.31 us -> 0.97 us
    div x1, other arithmetic: 1.31 us -> 0.53 us  [per_device(): return (departures, total[0:1] / jnp.sqrt(weight), total[1:2] / weight)]
where the time goes in v1:
time: 61.3 us; the launch traced here: 60.3 us
  Pallas kernels  58.2 us (95%)
  local copies, waits for them, and re-layouts  0.97 us (2%)
  between operations  0.64 us (1%)
    pallas_call x1, Pallas kernels, per_device(): pl.pallas_call(functools.partial(kernel, windows, regions, groups, slots,...  58.2 us

profile of v1, /device:TPU:8, one launch (start us, length us, event | category | flops | bytes accessed | tf_op | source)
XLA Modules:
  0.0 60.3 jit_solution(4360379276372699458)
XLA Ops:
  0.6 58.2 %shard_map.103 = (bf16[32,128,128]{2,1,0:T(8,128)(2,1)S(1)}, f32[8,128]{1,0:T(8,128)S(1)}) custom-call(bf16[1,16,256,128]{3,2,1,0:T(8,128)(2,1)} %traj.1, bf16[32,128,256]{2,1,0:T(8,128)(2,1)} %weights.1, bf16[32,128,128]{2,1,0:T(8,128)(2,1)} %observed.1, s32[32]{0:T(128)} %bitcast.2, s32[32]{0:T(128)} %blk_in.1, s32[32]{0:T(128)} %counts_in.1, ...), custom_call_target="tpu_custom_call" | custom-call | tf_op jit(solution)/shard_map/pallas_call | solution.py:220
  58.8 0.5 slice_divide_fusion
  59.3 1.0 %copy.12 = bf16[32,128,128]{2,1,0:T(8,128)(2,1)} copy(bf16[32,128,128]{2,1,0:T(8,128)(2,1)S(1)} %get-tuple-element.9) | data formatting | bytes 2097152

commit v2 on v1

--- a/solution.py
+++ b/solution.py
@@ -10,21 +10,19 @@
 GCAP = 4
 MESH = pl.DeviceIdType.MESH
 
+ASK = ((1, 2, 3, 4, 5, 6, 7), (2, 3, 1, 6), (4, 5, 6, 7, 1, 2, 3), (2, 3, 4, 5, 6, 7, 1))
+AHEAD_AFTER = (None, 6, 7, None)
+OUTER_GIVE, OUTER_TAKE = (1, 4, 5, 6, 7, 2, 3), (1, 2, 3, 6, 7, 4, 5)
+INNER_GIVE, INNER_LATE, INNER_TAKE = (2, 1, 3), (4, 5, 7, 6), ((1, 4, 5), (2, 3, 7, 6))
+ACROSS, AHEAD = 6, 4
+
 
 def flip(index, pattern):
-    bit = 1
-    moved = index
-    while bit <= pattern:
-        if pattern & bit:
-            moved = moved + bit * (1 - 2 * ((index // bit) % 2))
+    bit, moved = 1, index
+    while bit <= 64:
+        moved = moved + bit * ((pattern // bit) % 2) * (1 - 2 * ((index // bit) % 2))
         bit *= 2
     return moved
-
-
-def phases(windows):
-    half, quarter = windows // 2, max(1, windows // 4)
-    far = list(range(half, windows))
-    return far[:1] + list(range(quarter, half)) + far[1:] + list(range(1, quarter))
 
 
 def last_hits(win_of, value_of, groups, wanted, start):
@@ -40,15 +38,19 @@
     windows, regions, groups, slots, levels,
     traj, weights, observed, win_in, blk_in, counts_in, flags_in, inv_in,
     dep_out, total_out,
-    slab, wts, obs, send, recv, mask, dep_slot, dep_v, stat_send, stat_recv,
+    slab, wts, obs, send, recv, head, pre, on_out, on_in, mask, dep_slot, stat_send, stat_recv,
     idx, own, table, slot_tab, counts, flags, inv,
-    in_sems, out_sem, idx_send, idx_recv, dat_send, dat_recv, st_send, st_recv,
+    in_sems, ready_tm, ready_obs, idx_send, idx_recv, pass_send, dat_send, dat_recv,
+    pre_send, pre_recv, on_send, on_recv, st_send, st_recv,
 ):
     me = lax.axis_index("tm")
     my_region = lax.axis_index("obs")
     everyone = windows * regions
     flat = me * regions + my_region
-    order = phases(windows)
+    tuned = windows == 8
+    inner = ((me // 2 + 1) // 2) % 2 == 1
+    blocks, columns = slab.shape[0], slab.shape[1]
+    ahead = columns // AHEAD if tuned else 0
 
     small = [
         pltpu.make_async_copy(src, dst, in_sems.at[3 + n])
@@ -56,53 +58,153 @@
             ((win_in, own.at[0]), (blk_in, own.at[1]), (counts_in, counts), (flags_in, flags), (inv_in, inv))
         )
     ]
-    for copy in small:
-        copy.start()
     slab_in = pltpu.make_async_copy(traj.at[0], slab, in_sems.at[0])
-    slab_in.start()
+    head_in = pltpu.make_async_copy(traj.at[0, :, pl.ds(0, columns // AHEAD)], head, in_sems.at[8])
     wts_in = pltpu.make_async_copy(weights, wts, in_sems.at[1])
     obs_in = pltpu.make_async_copy(observed, obs, in_sems.at[2])
 
     barrier = pltpu.get_barrier_semaphore()
-
-    partners = [(flip(me, d), my_region) for d in order]
-    partners += [(me, (my_region + r) % regions) for r in range(1, regions)]
-    for partner in partners:
-        pl.semaphore_signal(barrier, inc=1, device_id=partner, device_id_type=MESH)
+    tm_peers = [(d, flip(me, d)) for d in range(1, windows)]
+    obs_peers = [(r, flip(my_region, r)) for r in range(2, regions)]
+    pl.semaphore_signal(barrier, inc=1, device_id=(me, flip(my_region, 1)), device_id_type=MESH)
+    for d, peer in tm_peers:
+        @pl.when(peer > me)
+        def _():
+            pl.semaphore_signal(barrier, inc=1, device_id=(peer, my_region), device_id_type=MESH)
+    for r, peer in obs_peers:
+        @pl.when(peer > my_region)
+        def _():
+            pl.semaphore_signal(barrier, inc=1, device_id=(me, peer), device_id_type=MESH)
+    small[0].start()
+    small[1].start()
+    if tuned:
+        head_in.start()
+    slab_in.start()
+    for copy in small[2:]:
+        copy.start()
+    pl.semaphore_wait(barrier, 1 + me + 2 * (my_region // 2))
+    for d, peer in tm_peers:
+        hears = peer < me
+        if tuned and d in (4, 5, 7):
+            hears = jnp.logical_and(hears, peer // 2 != 1)
+
+        @pl.when(hears)
+        def _():
+            pl.semaphore_signal(ready_tm.at[d - 1], inc=1, device_id=(peer, my_region), device_id_type=MESH)
+    for r, peer in obs_peers:
+        @pl.when(peer < my_region)
+        def _():
+            pl.semaphore_signal(ready_obs, inc=1, device_id=(me, peer), device_id_type=MESH)
     small[0].wait()
     small[1].wait()
-    pl.semaphore_wait(barrier, len(partners))
-
-    requests = []
-    for j, d in enumerate(order):
-        target = (flip(me, d), my_region)
-        copy = pltpu.make_async_remote_copy(
-            src_ref=own, dst_ref=idx.at[j],
-            send_sem=idx_send.at[j], recv_sem=idx_recv.at[j],
-            device_id=target, device_id_type=MESH,
-        )
-        copy.start()
-        requests.append(copy)
+
+    def request(d):
+        return pltpu.make_async_remote_copy(
+            src_ref=own, dst_ref=idx.at[d],
+            send_sem=idx_send, recv_sem=idx_recv.at[d - 1],
+            device_id=(flip(me, d), my_region), device_id_type=MESH,
+        )
+
+    def ask(d):
+        @pl.when(flip(me, d) > me)
+        def _():
+            pl.semaphore_wait(ready_tm.at[d - 1], 1)
+
+        request(d).start()
+
+    def pass_on(e):
+        return pltpu.make_async_remote_copy(
+            src_ref=idx.at[ACROSS], dst_ref=idx.at[e ^ ACROSS],
+            send_sem=pass_send, recv_sem=idx_recv.at[(e ^ ACROSS) - 1],
+            device_id=(flip(me, e), my_region), device_id_type=MESH,
+        )
+
+    def move(d, k, count=1, first=0):
+        part, rows = pl.ds(d * GCAP + k, count), pl.ds(first, columns - first)
+        return pltpu.make_async_remote_copy(
+            src_ref=send.at[part, rows], dst_ref=recv.at[part, rows],
+            send_sem=dat_send, recv_sem=dat_recv.at[d - 1 if d != ACROSS or k == 0 else windows - 2 + k],
+            device_id=(flip(me, d), my_region), device_id_type=MESH,
+        )
+
+    def moved(count):
+        part = send.at[pl.ds(0, count)]
+        pltpu.make_async_remote_copy(
+            src_ref=part, dst_ref=part, send_sem=dat_send, recv_sem=dat_recv.at[0],
+            device_id=(flip(me, 1), my_region), device_id_type=MESH,
+        ).wait_send()
+
+    def give(d, first=0, skip_heard=None):
+        if d != skip_heard:
+            request(d).wait_recv()
+        named = last_hits(lambda g: idx[d, 0, g], lambda g: idx[d, 1, g], groups, me, 0)
+        for k in range(GCAP):
+            send[d * GCAP + k, first:] = slab[named[k], first:]
+            move(d, k, 1, first).start()
+
+    def run_ahead():
+        return pltpu.make_async_remote_copy(
+            src_ref=head, dst_ref=pre, send_sem=pre_send, recv_sem=pre_recv,
+            device_id=(flip(me, ACROSS), my_region), device_id_type=MESH,
+        )
+
+    def hand_on(e):
+        return pltpu.make_async_remote_copy(
+            src_ref=on_out.at[e], dst_ref=on_in.at[e ^ ACROSS],
+            send_sem=on_send, recv_sem=on_recv.at[e % 2],
+            device_id=(flip(me, e), my_region), device_id_type=MESH,
+        )
+
+    def relay():
+        run_ahead().wait_recv()
+        for e in (1, 2, 3):
+            named = last_hits(
+                lambda g: idx[e, 0, g], lambda g: idx[e, 1, g], groups, flip(me, ACROSS), 0
+            )
+            for k in range(GCAP):
+                on_out[e, k] = pre[named[k]]
+            hand_on(e).start()
+
+    if tuned:
+        for z, order in enumerate(ASK):
+            @pl.when(me // 2 == z)
+            def _():
+                for d in order:
+                    ask(d)
+                    if d == AHEAD_AFTER[z]:
+                        head_in.wait()
+                        run_ahead().start()
+                if z in (0, 3):
+                    head_in.wait()
+                if z == 2:
+                    request(ACROSS).wait_recv()
+                    for e in (1, 2, 3):
+                        pass_on(e).start()
+    else:
+        for d in range(1, windows):
+            ask(d)
+    later = regions - 2 - 2 * (my_region // 2)
+
+    @pl.when(later > 0)
+    def _():
+        pl.semaphore_wait(ready_obs, later)
+
+    slab_in.wait()
     wts_in.start()
     obs_in.start()
-
-    slab_in.wait()
-    moves = []
-    for j, d in enumerate(order):
-        requests[j].wait_recv()
-        named = last_hits(
-            lambda g, j=j: idx[j, 0, g], lambda g, j=j: idx[j, 1, g], groups, me, 0
-        )
-        for k in range(GCAP):
-            send[j * GCAP + k] = slab[named[k]]
-        copy = pltpu.make_async_remote_copy(
-            src_ref=send.at[pl.ds(j * GCAP, GCAP)],
-            dst_ref=recv.at[pl.ds(j * GCAP, GCAP)],
-            send_sem=dat_send.at[j], recv_sem=dat_recv.at[j],
-            device_id=(flip(me, d), my_region), device_id_type=MESH,
-        )
-        copy.start()
-        moves.append(copy)
+    if tuned:
+        @pl.when(inner)
+        def _():
+            for d in INNER_GIVE:
+                give(d)
+
+        @pl.when(jnp.logical_not(inner))
+        def _():
+            for d in OUTER_GIVE:
+                give(d)
+    else:
+        for d in range(1, windows):
+            give(d)
 
     for copy in small[2:]:
         copy.wait()
@@ -170,40 +272,97 @@
             copy = pltpu.make_async_remote_copy(
                 src_ref=stat_send.at[w], dst_ref=stat_recv.at[flat],
                 send_sem=st_send, recv_sem=st_recv,
-                device_id=(w, (my_region + r) % regions), device_id_type=MESH,
+                device_id=(w, flip(my_region, r)), device_id_type=MESH,
             )
             copy.start()
 
     check(me, lambda k, g: slab[own[1, g]])
     share(me, 1)
-    for j, d in sorted(enumerate(order), key=lambda item: item[1] >= windows // 2):
+
+    def take(d, first=0):
         w = flip(me, d)
-        moves[j].wait_recv()
-        check(w, lambda k, g, j=j: recv[j * GCAP + k])
+        if first and d != ACROSS:
+            hand_on(d ^ ACROSS).wait_recv()
+
+        if d != ACROSS:
+            move(d, 0, GCAP, first).wait_recv()
+
+        def arrived(k, g):
+            if first:
+                recv[d * GCAP + k, :first] = pre[own[1, g]] if d == ACROSS else on_in[d, k]
+            if d == ACROSS:
+                move(d, k, 1, first).wait_recv()
+            return recv[d * GCAP + k]
+
+        check(w, arrived)
         share(w, 0)
 
+    if tuned:
+        @pl.when(inner)
+        def _():
+            for d in INNER_TAKE[0]:
+                take(d)
+            for d in INNER_LATE:
+                if d == ACROSS:
+                    @pl.when(me // 2 == 1)
+                    def _():
+                        request(ACROSS).wait_recv()
+                give(d, ahead, ACROSS)
+
+            relay()
+            for d in INNER_TAKE[1]:
+                take(d, ahead if d in (6, 7) else 0)
+            moved(len(INNER_GIVE) * GCAP + len(INNER_LATE) * GCAP * (columns - ahead) // columns)
+            run_ahead().wait_send()
+            part = on_out.at[pl.ds(1, 3)]
+            pltpu.make_async_remote_copy(
+                src_ref=part, dst_ref=part, send_sem=on_send, recv_sem=on_recv.at[0],
+                device_id=(flip(me, 1), my_region), device_id_type=MESH,
+            ).wait_send()
+
+        @pl.when(jnp.logical_not(inner))
+        def _():
+            for d in OUTER_TAKE:
+                take(d, ahead if d in (4, 5) else 0)
+            moved(len(OUTER_GIVE) * GCAP)
+    else:
+        for d in range(1, windows):
+            take(d)
+        moved((windows - 1) * GCAP)
+
     def permute(g, carry):
-        dep_v[g] = dep_slot[slot_tab[g]]
+        dep_out[g] = dep_slot[slot_tab[g]]
         return carry
 
     lax.fori_loop(0, groups, permute, 0, unroll=4)
-    dep_out[...] = dep_v[...]
-
-
-    for j in range(len(order)):
-        requests[j].wait_send()
-        moves[j].wait_send()
+
+    def asked(count, sem):
+        part = idx.at[pl.ds(0, count)]
+        pltpu.make_async_remote_copy(
+            src_ref=part, dst_ref=part, send_sem=sem, recv_sem=idx_recv.at[0],
+            device_id=(flip(me, 1), my_region), device_id_type=MESH,
+        ).wait_send()
+
+    if tuned:
+        for z, order in enumerate(ASK):
+            @pl.when(me // 2 == z)
+            def _():
+                asked(len(order), idx_send)
+                if z == 2:
+                    asked(3, pass_send)
+    else:
+        asked(windows - 1, idx_send)
 
     rest = pl.ds(0, everyone - 1)
-    arrived = pltpu.make_async_remote_copy(
+    everything = pltpu.make_async_remote_copy(
         src_ref=stat_recv.at[rest], dst_ref=stat_recv.at[rest],
         send_sem=st_send, recv_sem=st_recv,
         device_id=(flip(me, 1), my_region), device_id_type=MESH,
     )
-    arrived.wait_recv()
+    everything.wait_recv()
     stat_recv[flat] = stat_send[me]
     total_out[...] = jnp.sum(stat_recv[...], 0)
-    arrived.wait_send()
+    everything.wait_send()
 
 
 def per_device(trajectory, weights, observed, window, block, counts, flags, inv_error):
@@ -212,8 +371,8 @@
     groups, slots, columns = weights.shape
     levels = observed.shape[2]
     blocks = trajectory.shape[1]
-    peers = windows - 1
     dma = pltpu.SemaphoreType.DMA
+    regular = pltpu.SemaphoreType.REGULAR
     hbm = pl.BlockSpec(memory_space=pl.ANY)
     vmem = pl.BlockSpec(memory_space=pltpu.VMEM)
     b16, f32, i32 = jnp.bfloat16, jnp.float32, jnp.int32
@@ -229,26 +388,35 @@
             pltpu.VMEM((blocks, columns, levels), b16),
             pltpu.VMEM((groups, slots, columns), b16),
             pltpu.VMEM((groups, slots, levels), b16),
-            pltpu.VMEM((peers * GCAP, columns, levels), b16),
-            pltpu.VMEM((peers * GCAP, columns, levels), b16),
+            pltpu.VMEM((windows * GCAP, columns, levels), b16),
+            pltpu.VMEM((windows * GCAP, columns, levels), b16),
+            pltpu.VMEM((blocks, columns // AHEAD, levels), b16),
+            pltpu.VMEM((blocks, columns // AHEAD, levels), b16),
+            pltpu.VMEM((windows, GCAP, columns // AHEAD, levels), b16),
+            pltpu.VMEM((windows, GCAP, columns // AHEAD, levels), b16),
             pltpu.VMEM((groups, slots, levels), f32),
             pltpu.VMEM((windows * GCAP, slots, levels), b16),
-            pltpu.VMEM((groups, slots, levels), b16),
             pltpu.VMEM((windows, 8, levels), f32),
             pltpu.VMEM((windows * regions, 8, levels), f32),
-            pltpu.SMEM((peers, 2, groups), i32),
+            pltpu.SMEM((windows, 2, groups), i32),
             pltpu.SMEM((2, groups), i32),
             pltpu.SMEM((windows * GCAP,), i32),
             pltpu.SMEM((groups,), i32),
             pltpu.SMEM((groups,), i32),
             pltpu.VMEM((groups, slots), i32),
             pltpu.VMEM((1, levels), f32),
-            dma((8,)),
-            dma,
-            dma((peers,)),
-            dma((peers,)),
-            dma((peers,)),
-            dma((peers,)),
+            dma((9,)),
+            regular((windows - 1,)),
+            regular,
+            dma,
+            dma((windows - 1,)),
+            dma,
+            dma,
+            dma((windows + GCAP - 2,)),
+            dma,
+            dma,
+            dma,
+            dma((2,)),
             dma,
             dma,
         ],

time: 61.3 us -> 58.4 us (0.953)
  Pallas kernels: 58.2 us -> 55.8 us
    pallas_call x1, Pallas kernels: 58.2 us -> 55.8 us  [per_device(): pl.pallas_call(functools.partial(kernel, windows, regions, groups, slots,...]
where the time goes in v2:
time: 58.4 us; the launch traced here: 57.9 us
  Pallas kernels  55.8 us (96%)
  local copies, waits for them, and re-layouts  0.97 us (2%)
  between operations  0.64 us (1%)
    pallas_call x1, Pallas kernels, per_device(): pl.pallas_call(functools.partial(kernel, windows, regions, groups, slots,...  55.8 us

profile of v2, /device:TPU:8, one launch (start us, length us, event | category | flops | bytes accessed | tf_op | source)
XLA Modules:
  0.0 57.9 jit_solution(5144491867259826050)
XLA Ops:
  0.6 55.8 %shard_map.103 = (bf16[32,128,128]{2,1,0:T(8,128)(2,1)S(1)}, f32[8,128]{1,0:T(8,128)S(1)}) custom-call(bf16[1,16,256,128]{3,2,1,0:T(8,128)(2,1)} %traj.1, bf16[32,128,256]{2,1,0:T(8,128)(2,1)} %weights.1, bf16[32,128,128]{2,1,0:T(8,128)(2,1)} %observed.1, s32[32]{0:T(128)} %bitcast.2, s32[32]{0:T(128)} %blk_in.1, s32[32]{0:T(128)} %counts_in.1, ...), custom_call_target="tpu_custom_call" | custom-call | tf_op jit(solution)/shard_map/pallas_call | solution.py:379
  56.4 0.5 slice_divide_fusion
  57.0 1.0 %copy.12 = bf16[32,128,128]{2,1,0:T(8,128)(2,1)} copy(bf16[32,128,128]{2,1,0:T(8,128)(2,1)S(1)} %get-tuple-element.9) | data formatting | bytes 2097152

commit v3 on v2

--- a/solution.py
+++ b/solution.py
@@ -10,8 +10,8 @@
 GCAP = 4
 MESH = pl.DeviceIdType.MESH
 
-ASK = ((1, 2, 3, 4, 5, 6, 7), (2, 3, 1, 6), (4, 5, 6, 7, 1, 2, 3), (2, 3, 4, 5, 6, 7, 1))
-AHEAD_AFTER = (None, 6, 7, None)
+ASK = ((1, 2, 3, 4, 5, 6, 7), (6, 2, 3, 1), (4, 5, 7, 6, 1, 2, 3), (2, 3, 4, 5, 6, 7, 1))
+AHEAD_AFTER = (None, 6, 6, None)
 OUTER_GIVE, OUTER_TAKE = (1, 4, 5, 6, 7, 2, 3), (1, 2, 3, 6, 7, 4, 5)
 INNER_GIVE, INNER_LATE, INNER_TAKE = (2, 1, 3), (4, 5, 7, 6), ((1, 4, 5), (2, 3, 7, 6))
 ACROSS, AHEAD = 6, 4
@@ -48,7 +48,8 @@
     everyone = windows * regions
     flat = me * regions + my_region
     tuned = windows == 8
-    inner = ((me // 2 + 1) // 2) % 2 == 1
+    inner_flag = ((me // 2 + 1) // 2) % 2
+    inner = inner_flag == 1
     blocks, columns = slab.shape[0], slab.shape[1]
     ahead = columns // AHEAD if tuned else 0
 
@@ -64,11 +65,18 @@
     obs_in = pltpu.make_async_copy(observed, obs, in_sems.at[2])
 
     barrier = pltpu.get_barrier_semaphore()
+
+    def greets(d):
+        before = flip(me, d) > me
+        if tuned and d == ACROSS:
+            return jnp.logical_xor(before, inner)
+        return before
+
     tm_peers = [(d, flip(me, d)) for d in range(1, windows)]
     obs_peers = [(r, flip(my_region, r)) for r in range(2, regions)]
     pl.semaphore_signal(barrier, inc=1, device_id=(me, flip(my_region, 1)), device_id_type=MESH)
     for d, peer in tm_peers:
-        @pl.when(peer > me)
+        @pl.when(greets(d))
         def _():
             pl.semaphore_signal(barrier, inc=1, device_id=(peer, my_region), device_id_type=MESH)
     for r, peer in obs_peers:
@@ -82,9 +90,12 @@
     slab_in.start()
     for copy in small[2:]:
         copy.start()
-    pl.semaphore_wait(barrier, 1 + me + 2 * (my_region // 2))
+    early = 1 + me + 2 * (my_region // 2)
+    if tuned:
+        early = early + inner_flag * (3 - 2 * (me // 2))
+    pl.semaphore_wait(barrier, early)
     for d, peer in tm_peers:
-        hears = peer < me
+        hears = jnp.logical_not(greets(d))
         if tuned and d in (4, 5, 7):
             hears = jnp.logical_and(hears, peer // 2 != 1)
 
@@ -106,7 +117,7 @@
         )
 
     def ask(d):
-        @pl.when(flip(me, d) > me)
+        @pl.when(greets(d))
         def _():
             pl.semaphore_wait(ready_tm.at[d - 1], 1)
 
@@ -140,7 +151,10 @@
         named = last_hits(lambda g: idx[d, 0, g], lambda g: idx[d, 1, g], groups, me, 0)
         for k in range(GCAP):
             send[d * GCAP + k, first:] = slab[named[k], first:]
-            move(d, k, 1, first).start()
+            if d == ACROSS:
+                move(d, k, 1, first).start()
+        if d != ACROSS:
+            move(d, 0, GCAP, first).start()
 
     def run_ahead():
         return pltpu.make_async_remote_copy(
@@ -268,7 +282,7 @@
         )
 
     def share(w, first):
-        for r in range(first, regions):
+        for r in reversed(range(first, regions)):
             copy = pltpu.make_async_remote_copy(
                 src_ref=stat_send.at[w], dst_ref=stat_recv.at[flat],
                 send_sem=st_send, recv_sem=st_recv,
@@ -363,6 +377,21 @@
     stat_recv[flat] = stat_send[me]
     total_out[...] = jnp.sum(stat_recv[...], 0)
     everything.wait_send()
+
+
+def finish(dep, total, dep_out, bias_out, chi_out, ratio, sems):
+    whole = pltpu.make_async_copy(dep, dep_out, sems.at[0])
+    whole.start()
+    weight = total[2:3] + 1.0
+    ratio[0:1] = total[0:1] / jnp.sqrt(weight)
+    ratio[8:9] = total[1:2] / weight
+    bias = pltpu.make_async_copy(ratio.at[0:1], bias_out, sems.at[1])
+    chi = pltpu.make_async_copy(ratio.at[8:9], chi_out, sems.at[2])
+    bias.start()
+    chi.start()
+    bias.wait()
+    chi.wait()
+    whole.wait()
 
 
 def per_device(trajectory, weights, observed, window, block, counts, flags, inv_error):
@@ -427,8 +456,17 @@
         trajectory, weights, observed, window[:, 0], block, counts, flags,
         inv_error.reshape(1, levels),
     )
-    weight = total[2:3] + 1.0
-    return (departures, total[0:1] / jnp.sqrt(weight), total[1:2] / weight)
+    return pl.pallas_call(
+        finish,
+        out_shape=(
+            jax.ShapeDtypeStruct((groups, slots, levels), b16),
+            jax.ShapeDtypeStruct((1, levels), f32),
+            jax.ShapeDtypeStruct((1, levels), f32),
+        ),
+        in_specs=[vmem, vmem],
+        out_specs=(hbm, hbm, hbm),
+        scratch_shapes=[pltpu.VMEM((16, levels), f32), dma((3,))],
+    )(*(pltpu.with_memory_space_constraint(x, pltpu.VMEM) for x in (departures, total)))
 
 
 def solution(mesh):

time: 58.4 us -> 56.9 us (0.974)
  local copies, waits for them, and re-layouts: 0.97 us -> 0 us
    pallas_call x0 -> x1, Pallas kernels: none -> 1 us  [per_device(): pl.pallas_call(finish, out_shape=(jax.ShapeDtypeStruct((groups, slots, le...]
    unnamed x1 -> x0, local copies, waits for them, and re-layouts: 0.97 us -> none
    pallas_call x1, Pallas kernels: 55.8 us -> 55.1 us  [per_device(): pl.pallas_call(functools.partial(kernel, windows, regions, groups, slots,...]
where the time goes in v3:
time: 56.9 us; the launch traced here: 56.7 us
  Pallas kernels  56.1 us (99%)
  between operations  0.64 us (1%)
    pallas_call x1, Pallas kernels, per_device(): pl.pallas_call(functools.partial(kernel, windows, regions, groups, slots,...  55.1 us

profile of v3, /device:TPU:8, one launch (start us, length us, event | category | flops | bytes accessed | tf_op | source)
XLA Modules:
  0.0 56.7 jit_solution(8121731310979973371)
XLA Ops:
  0.6 55.1 %shard_map.103 = (bf16[32,128,128]{2,1,0:T(8,128)(2,1)S(1)}, f32[8,128]{1,0:T(8,128)S(1)}) custom-call(bf16[1,16,256,128]{3,2,1,0:T(8,128)(2,1)} %traj.1, bf16[32,128,256]{2,1,0:T(8,128)(2,1)} %weights.1, bf16[32,128,128]{2,1,0:T(8,128)(2,1)} %observed.1, s32[32]{0:T(128)} %bitcast.2, s32[32]{0:T(128)} %blk_in.1, s32[32]{0:T(128)} %counts_in.1, ...), custom_call_target="tpu_custom_call" | custom-call | tf_op jit(solution)/shard_map/pallas_call | solution.py:408
  55.7 1.0 %shard_map.104 = (bf16[32,128,128]{2,1,0:T(8,128)(2,1)}, f32[1,128]{1,0:T(1,128)}, f32[1,128]{1,0:T(1,128)}) custom-call(bf16[32,128,128]{2,1,0:T(8,128)(2,1)S(1)} %get-tuple-element.5.dep, f32[8,128]{1,0:T(8,128)S(1)} %get-tuple-element.6.total), custom_call_target="tpu_custom_call" | custom-call | tf_op jit(solution)/shard_map/pallas_call | solution.py:459

commit v4 on v3

--- a/solution.py
+++ b/solution.py
@@ -12,8 +12,8 @@
 
 ASK = ((1, 2, 3, 4, 5, 6, 7), (6, 2, 3, 1), (4, 5, 7, 6, 1, 2, 3), (2, 3, 4, 5, 6, 7, 1))
 AHEAD_AFTER = (None, 6, 6, None)
-OUTER_GIVE, OUTER_TAKE = (1, 4, 5, 6, 7, 2, 3), (1, 2, 3, 6, 7, 4, 5)
-INNER_GIVE, INNER_LATE, INNER_TAKE = (2, 1, 3), (4, 5, 7, 6), ((1, 4, 5), (2, 3, 7, 6))
+OUTER_GIVE, OUTER_TAKE = (1, 5, 4, 7, 6, 3, 2), (1, 2, 3, 7, 6, 4, 5)
+INNER_GIVE, INNER_LATE, INNER_TAKE = (2, 3, 1), (4, 5, 7, 6), ((1, 5, 4), (3, 2, 7, 6))
 ACROSS, AHEAD = 6, 4
 
 
@@ -66,17 +66,14 @@
 
     barrier = pltpu.get_barrier_semaphore()
 
-    def greets(d):
-        before = flip(me, d) > me
-        if tuned and d == ACROSS:
-            return jnp.logical_xor(before, inner)
-        return before
+    def opposite(d):
+        return jnp.logical_and(inner, tuned and d == ACROSS)
 
     tm_peers = [(d, flip(me, d)) for d in range(1, windows)]
     obs_peers = [(r, flip(my_region, r)) for r in range(2, regions)]
     pl.semaphore_signal(barrier, inc=1, device_id=(me, flip(my_region, 1)), device_id_type=MESH)
     for d, peer in tm_peers:
-        @pl.when(greets(d))
+        @pl.when(jnp.logical_or(peer > me, opposite(d)))
         def _():
             pl.semaphore_signal(barrier, inc=1, device_id=(peer, my_region), device_id_type=MESH)
     for r, peer in obs_peers:
@@ -92,10 +89,10 @@
         copy.start()
     early = 1 + me + 2 * (my_region // 2)
     if tuned:
-        early = early + inner_flag * (3 - 2 * (me // 2))
+        early = early + inner_flag * (2 - me // 2)
     pl.semaphore_wait(barrier, early)
     for d, peer in tm_peers:
-        hears = jnp.logical_not(greets(d))
+        hears = jnp.logical_and(peer < me, jnp.logical_not(opposite(d)))
         if tuned and d in (4, 5, 7):
             hears = jnp.logical_and(hears, peer // 2 != 1)
 
@@ -117,7 +114,7 @@
         )
 
     def ask(d):
-        @pl.when(greets(d))
+        @pl.when(jnp.logical_and(flip(me, d) > me, jnp.logical_not(opposite(d))))
         def _():
             pl.semaphore_wait(ready_tm.at[d - 1], 1)
 
@@ -277,9 +274,7 @@
             one = one + jnp.sum(dep, 0, keepdims=True)
             two = two + jnp.sum(dep * dep, 0, keepdims=True)
             kept = kept + jnp.sum(keep, 0, keepdims=True)
-        stat_send[w] = jnp.concatenate(
-            [one, two, kept, jnp.zeros((5, levels), jnp.float32)], 0
-        )
+        stat_send[w] = jnp.concatenate([one, two, kept] + [kept] * (stat_send.shape[1] - 3), 0)
 
     def share(w, first):
         for r in reversed(range(first, regions)):
@@ -409,7 +404,7 @@
         functools.partial(kernel, windows, regions, groups, slots, levels),
         out_shape=(
             pltpu.VMEM((groups, slots, levels), b16),
-            pltpu.VMEM((8, levels), f32),
+            pltpu.VMEM((3, levels), f32),
         ),
         in_specs=[hbm] * 8,
         out_specs=(vmem, vmem),
@@ -425,8 +420,8 @@
             pltpu.VMEM((windows, GCAP, columns // AHEAD, levels), b16),
             pltpu.VMEM((groups, slots, levels), f32),
             pltpu.VMEM((windows * GCAP, slots, levels), b16),
-            pltpu.VMEM((windows, 8, levels), f32),
-            pltpu.VMEM((windows * regions, 8, levels), f32),
+            pltpu.VMEM((windows, 3, levels), f32),
+            pltpu.VMEM((windows * regions, 3, levels), f32),
             pltpu.SMEM((windows, 2, groups), i32),
             pltpu.SMEM((2, groups), i32),
             pltpu.SMEM((windows * GCAP,), i32),

time: 56.9 us -> 54.9 us (0.965)
  Pallas kernels: 56.1 us -> 54.1 us
    pallas_call x1, Pallas kernels: 55.1 us -> 53.1 us  [per_device(): pl.pallas_call(functools.partial(kernel, windows, regions, groups, slots,...]
where the time goes in v4:
time: 54.9 us; the launch traced here: 54.8 us
  Pallas kernels  54.1 us (99%)
  between operations  0.64 us (1%)
    pallas_call x1, Pallas kernels, per_device(): pl.pallas_call(functools.partial(kernel, windows, regions, groups, slots,...  53.1 us

profile of v4, /device:TPU:8, one launch (start us, length us, event | category | flops | bytes accessed | tf_op | source)
XLA Modules:
  0.0 54.8 jit_solution(16173176866663397532)
XLA Ops:
  0.6 53.1 %shard_map.103 = (bf16[32,128,128]{2,1,0:T(8,128)(2,1)S(1)}, f32[3,128]{1,0:T(4,128)S(1)}) custom-call(bf16[1,16,256,128]{3,2,1,0:T(8,128)(2,1)} %traj.1, bf16[32,128,256]{2,1,0:T(8,128)(2,1)} %weights.1, bf16[32,128,128]{2,1,0:T(8,128)(2,1)} %observed.1, s32[32]{0:T(128)} %bitcast.2, s32[32]{0:T(128)} %blk_in.1, s32[32]{0:T(128)} %counts_in.1, ...), custom_call_target="tpu_custom_call" | custom-call | tf_op jit(solution)/shard_map/pallas_call | solution.py:403
  53.8 1.0 %shard_map.104 = (bf16[32,128,128]{2,1,0:T(8,128)(2,1)}, f32[1,128]{1,0:T(1,128)}, f32[1,128]{1,0:T(1,128)}) custom-call(bf16[32,128,128]{2,1,0:T(8,128)(2,1)S(1)} %get-tuple-element.5.dep, f32[3,128]{1,0:T(4,128)S(1)} %get-tuple-element.6.total), custom_call_target="tpu_custom_call" | custom-call | tf_op jit(solution)/shard_map/pallas_call | solution.py:454

commit v5 on v4

--- a/solution.py
+++ b/solution.py
@@ -12,8 +12,8 @@
 
 ASK = ((1, 2, 3, 4, 5, 6, 7), (6, 2, 3, 1), (4, 5, 7, 6, 1, 2, 3), (2, 3, 4, 5, 6, 7, 1))
 AHEAD_AFTER = (None, 6, 6, None)
-OUTER_GIVE, OUTER_TAKE = (1, 5, 4, 7, 6, 3, 2), (1, 2, 3, 7, 6, 4, 5)
-INNER_GIVE, INNER_LATE, INNER_TAKE = (2, 3, 1), (4, 5, 7, 6), ((1, 5, 4), (3, 2, 7, 6))
+OUTER_GIVE, OUTER_TAKE = (5, 4, 1, 7, 6, 3, 2), (1, 2, 3, 7, 6, 4, 5)
+INNER_GIVE, INNER_LATE, INNER_TAKE = (1, 2, 3), (4, 5, 7, 6), ((1, 5, 4), (3, 2, 7, 6))
 ACROSS, AHEAD = 6, 4
 
 

time: 54.9 us -> 54.9 us (level)
  no operation moved by 1% of the time
where the time goes in v5:
time: 54.9 us; the launch traced here: 54.8 us
  Pallas kernels  54.1 us (99%)
  between operations  0.64 us (1%)
    pallas_call x1, Pallas kernels, per_device(): pl.pallas_call(functools.partial(kernel, windows, regions, groups, slots,...  53.1 us

profile of v5, /device:TPU:8, one launch (start us, length us, event | category | flops | bytes accessed | tf_op | source)
XLA Modules:
  0.0 54.8 jit_solution(18207473006669302830)
XLA Ops:
  0.6 53.1 %shard_map.103 = (bf16[32,128,128]{2,1,0:T(8,128)(2,1)S(1)}, f32[3,128]{1,0:T(4,128)S(1)}) custom-call(bf16[1,16,256,128]{3,2,1,0:T(8,128)(2,1)} %traj.1, bf16[32,128,256]{2,1,0:T(8,128)(2,1)} %weights.1, bf16[32,128,128]{2,1,0:T(8,128)(2,1)} %observed.1, s32[32]{0:T(128)} %bitcast.2, s32[32]{0:T(128)} %blk_in.1, s32[32]{0:T(128)} %counts_in.1, ...), custom_call_target="tpu_custom_call" | custom-call | tf_op jit(solution)/shard_map/pallas_call | solution.py:403
  53.8 1.0 %shard_map.104 = (bf16[32,128,128]{2,1,0:T(8,128)(2,1)}, f32[1,128]{1,0:T(1,128)}, f32[1,128]{1,0:T(1,128)}) custom-call(bf16[32,128,128]{2,1,0:T(8,128)(2,1)S(1)} %get-tuple-element.5.dep, f32[3,128]{1,0:T(4,128)S(1)} %get-tuple-element.6.total), custom_call_target="tpu_custom_call" | custom-call | tf_op jit(solution)/shard_map/pallas_call | solution.py:454
